TPU v7x, 32 devices: a whole 2x2x4 slice. The times are simulated.
32 devices in a mesh: groups: 2 (over y), seq: 4 (over z), head: 4 (over x, core).
Axes of the slice: x: 2, y: 2, z: 4, core: 2. Of those that a mesh axis runs over, the one named last changes fastest.
Arguments:
- queries: bfloat16 [2048, 8192], P(('groups', 'seq'), 'head'), parts along dimension 0, may hold values from -16 to 16
- keys: bfloat16 [2048, 1024], P(('groups', 'seq'), 'head'), parts along dimension 0, may hold values from -16 to 16
- values: bfloat16 [2048, 1024], P(('groups', 'seq'), 'head'), parts along dimension 0, may hold values from -6 to 6
- prompt_len: int32 [2], P('groups'), parts along dimension 0, may hold values from 256 to 1024
- page_dest: int32 [8, 2], P('groups'), parts along dimension 0, may hold values from 0 to 3, all different within a row; in each aligned block of 4 rows (0 to 3, 4 to 7, ...) at most 4 rows name the same one
Outputs:
- attended: bfloat16 [2048, 8192], P(('groups', 'seq'), 'head'), parts along dimension 0
- decode_page_cache: bfloat16 [32, 128, 2048], P(('groups', 'seq'), None, 'head'), parts along dimension 0
There are 2 independent parts, one for each index of `groups`. A program takes and returns all parts, laid end to end along the dimension named above; each array names one. Nothing has to cross between parts.
Inputs may be any that keep to these rules, and one draw needn't show every extreme that they name: `page_dest`: row s names the decode devices of the 2 pages of tokens s * 256 to (s + 1) * 256 - 1, all different within a row; no device is named more than 4 times in all, and some device exactly 4 times.
All inputs are finite; a program needn't handle non-finite values.
Results may differ from a plain program's by a relative error of at most 0.005.
Values may be sent and summed in bfloat16 or wider, within the bound.
A program may use at most 64 MiB of HBM per device.

v0:
```python
import math
import jax
import jax.numpy as jnp
from jax import lax
from jax.sharding import PartitionSpec as P

HEAD_SIZE = 128
PAGE_TOKENS = 128
NEG_FILL = -1e30


def blank_state(kv_heads, group_size, query_count):
    return (
        jnp.full((kv_heads, group_size, query_count), NEG_FILL, jnp.float32),
        jnp.zeros((kv_heads, group_size, query_count), jnp.float32),
        jnp.zeros((kv_heads, group_size, query_count, HEAD_SIZE), jnp.float32),
    )


def attend_block(
    query_state, query_block, query_pos, key_block, value_block, block_start, prompt_end
):
    key_count = key_block.shape[0]
    kv_heads = key_block.shape[1] // HEAD_SIZE
    keys_split = key_block.reshape(key_count, kv_heads, HEAD_SIZE)
    values_split = value_block.reshape(key_count, kv_heads, HEAD_SIZE)
    scores = jnp.einsum(
        "rkgd,pkd->kgrp", query_block, keys_split, preferred_element_type=jnp.float32
    )
    scores = scores * (1.0 / math.sqrt(HEAD_SIZE))
    key_pos = block_start + jnp.arange(key_count, dtype=jnp.int32)
    allowed = (key_pos[None, :] <= query_pos[:, None]) & (key_pos[None, :] < prompt_end)
    scores = jnp.where(allowed, scores, NEG_FILL)
    old_max = query_state[0]
    new_max = jnp.maximum(old_max, jnp.max(scores, axis=-1))
    weights = jnp.where(allowed, jnp.exp(scores - new_max[..., None]), 0.0)
    factor = jnp.exp(old_max - new_max)
    denominator = query_state[1] * factor + jnp.sum(weights, axis=-1)
    accumulated = query_state[2] * factor[..., None] + jnp.einsum(
        "kgrp,pkd->kgrd",
        weights.astype(jnp.bfloat16),
        values_split,
        preferred_element_type=jnp.float32,
    )
    return (new_max, denominator, accumulated)


def finish(query_state, query_pos, prompt_end):
    query_live = query_pos < prompt_end
    safe_total = jnp.where(query_live[None, None, :], query_state[1], 1.0)
    result = jnp.where(query_live[None, None, :, None], query_state[2] / safe_total[..., None], 0.0)
    query_count = query_pos.shape[0]
    return result.transpose(2, 0, 1, 3).reshape(query_count, -1).astype(jnp.bfloat16)


def join_pages(key_rows, value_rows):
    page_count = key_rows.shape[0] // PAGE_TOKENS
    kv_heads = key_rows.shape[1] // HEAD_SIZE
    stacked = jnp.stack(
        (
            key_rows.reshape(page_count, PAGE_TOKENS, kv_heads, HEAD_SIZE),
            value_rows.reshape(page_count, PAGE_TOKENS, kv_heads, HEAD_SIZE),
        ),
        axis=3,
    )
    return stacked.reshape(page_count, PAGE_TOKENS, 2 * key_rows.shape[1])


def slot_pages(page_dest, owner, slots):
    flat_dest = page_dest.reshape(-1)
    page_order = jnp.arange(flat_dest.shape[0], dtype=jnp.int32)
    same_dest = flat_dest[:, None] == flat_dest[None, :]
    dest_rank = jnp.sum(same_dest & (page_order[None, :] < page_order[:, None]), axis=1)
    matched = (flat_dest[:, None] == owner) & (
        dest_rank[:, None] == jnp.arange(slots, dtype=jnp.int32)[None, :]
    )
    page_index = jnp.sum(jnp.where(matched, page_order[:, None], 0), axis=0)
    present = jnp.any(matched, axis=0)
    return (flat_dest, page_index, present)


def place_pages(stored, key_block, value_block, block_start, prompt_end, page_index, present):
    key_pos = block_start + jnp.arange(key_block.shape[0], dtype=jnp.int32)
    token_present = (key_pos < prompt_end)[:, None]
    block_pages = join_pages(
        jnp.where(token_present, key_block, 0), jnp.where(token_present, value_block, 0)
    )
    page_count = block_pages.shape[0]
    local_index = page_index - block_start // PAGE_TOKENS
    inside = present & (local_index >= 0) & (local_index < page_count)
    picked = block_pages[jnp.clip(local_index, 0, page_count - 1)]
    return jnp.where(inside[:, None, None], picked, stored)


def local(queries, keys, values, prompt_len, page_dest):
    shard_rows = queries.shape[0]
    kv_width = keys.shape[1]
    kv_heads = kv_width // HEAD_SIZE
    group_size = queries.shape[1] // kv_width
    seq_index = lax.axis_index("seq")
    prompt_end = prompt_len[0]
    per_device = page_dest.shape[1]
    slots = 2 * per_device
    flat_dest, page_index, present = slot_pages(page_dest, seq_index, slots)
    own_rows = seq_index * shard_rows + jnp.arange(shard_rows, dtype=jnp.int32)
    query_parts = (queries,)
    positions = (own_rows,)
    shaped = tuple(
        (
            part_rows.reshape(part_rows.shape[0], kv_heads, group_size, HEAD_SIZE)
            for part_rows in query_parts
        )
    )
    states = tuple(
        (blank_state(kv_heads, group_size, part_rows.shape[0]) for part_rows in query_parts)
    )
    page_store = jnp.zeros((slots, PAGE_TOKENS, 2 * kv_width), jnp.bfloat16)
    key_piece = lax.all_gather(keys, "seq", axis=0, tiled=True)
    value_piece = lax.all_gather(values, "seq", axis=0, tiled=True)
    block_count = key_piece.shape[0] // shard_rows
    per_step = max(1, min(block_count, 512 // shard_rows))
    while block_count % per_step:
        per_step -= 1
    step_rows = per_step * shard_rows
    steps_count = block_count // per_step
    key_blocks = key_piece.reshape(steps_count, step_rows, kv_width)
    value_blocks = value_piece.reshape(steps_count, step_rows, kv_width)

    def one_block(inner_carry, block_item):
        block_states, stored = inner_carry
        key_block, value_block, number = block_item
        block_start = number * step_rows
        updated = []
        for query_state, query_block, query_pos in zip(block_states, shaped, positions):
            needed = block_start <= jnp.minimum(query_pos[-1], prompt_end - 1)
            updated.append(
                lax.cond(
                    needed,
                    lambda kept: attend_block(
                        kept,
                        query_block,
                        query_pos,
                        key_block,
                        value_block,
                        block_start,
                        prompt_end,
                    ),
                    lambda kept: kept,
                    query_state,
                )
            )
        stored = place_pages(
            stored, key_block, value_block, block_start, prompt_end, page_index, present
        )
        return ((tuple(updated), stored), None)

    result, unused = lax.scan(
        one_block,
        (states, page_store),
        (key_blocks, value_blocks, jnp.arange(steps_count, dtype=jnp.int32)),
    )
    final_states, stored = result
    outputs = [
        finish(query_state, query_pos, prompt_end)
        for query_state, query_pos in zip(final_states, positions)
    ]
    attended = outputs[0]
    return (attended, stored)


def solution(mesh):
    return jax.shard_map(
        local,
        mesh=mesh,
        in_specs=(
            P(("groups", "seq"), "head"),
            P(("groups", "seq"), "head"),
            P(("groups", "seq"), "head"),
            P("groups"),
            P("groups", None),
        ),
        out_specs=(P(("groups", "seq"), "head"), P(("groups", "seq"), None, "head")),
        check_vma=False,
    )
```

profile of v0, /device:TPU:26, one launch (start us, length us, event | category | flops | bytes accessed | tf_op | source)
XLA Modules:
  0.0 76.9 jit_solution(3035175965505265752)
XLA Ops:
  2.7 0.8 copy.34
  4.0 16.3 %all_gather.6 = bf16[1024,256]{1,0:T(8,128)(2,1)} all-gather(bf16[256,256]{1,0:T(8,128)(2,1)} %param.10), channel_id=1, replica_groups=mesh['groups'=2,'seq'=4,'head'=4] {'seq'}, dimensions={0}, use_global_device_ids=true | all-gather | bytes 655360 | tf_op jit(solution)/shard_map/all_gather | solution.py:118
  20.3 16.4 %all_gather.7 = bf16[1024,256]{1,0:T(8,128)(2,1)} all-gather(bf16[256,256]{1,0:T(8,128)(2,1)} %param.11), channel_id=1, replica_groups=mesh['groups'=2,'seq'=4,'head'=4] {'seq'}, dimensions={0}, use_global_device_ids=true | all-gather | bytes 655360 | tf_op jit(solution)/shard_map/all_gather | solution.py:119
  36.7 1.5 %copy.33 = bf16[256,2048]{0,1:T(8,128)(2,1)S(1)} copy(bf16[256,2048]{1,0:T(8,128)(2,1)} %param.9) | data formatting | bytes 2097152 | tf_op args[0]
  38.9 1.6 %broadcast_in_dim.106 = f32[2,8,256,128]{3,2,1,0:T(8,128)} broadcast(f32[]{:T(128)} %constant.102.clone.1), dimensions={} | broadcast | bytes 2097156 | tf_op jit(solution)/shard_map/broadcast_in_dim | solution.py:16
  40.4 31.5 %while.20 = (s32[]{:T(128)}, f32[2,8,256]{2,1,0:T(8,128)S(1)}, f32[2,8,256]{2,1,0:T(8,128)S(1)}, f32[2,8,256,128]{3,2,1,0:T(8,128)}, bf16[4,128,512]{1,2,0:T(8,1...) while((s32[]{:T(128)}, f32[2,8,256]{2,1,0:T(8,128)S(1)}, ...), condition=%wide.region_8.9_spmd.clone, body=%wide.region_3.8_spmd.clone.sunk | while | flops 1103377152 | bytes 57424572 | solution.py:157
  42.5 1.1 %constant_dynamic-slice_fusion.3 = (bf16[1,512,256]{2,1,0:T(8,128)(2,1)S(1)}, bf16[1,512,256]{2,1,0:T(8,128)(2,1)S(1)}) fusion(bf16[2,512,256]{2,1,0:T(8,128)(2,1)} %get-tuple-element.556, s32[]{:T(128)S(6)} %copy.67, bf16[2,512,256]{2,1,0:T(8,128)(2,1)} %get-tuple-element.555), kind=kLoop, calls=%fused_computation.31.clone.1 | loop fusion | bytes 1048580 | tf_op jit(solution)/shard_map/while/body/jit(dynamic_index_in_dim)/dynamic_slice | solution.py:157
  43.8 1.1 %broadcast_select_fusion.4 = (bf16[4,128,2,1,128]{4,2,1,0,3:T(2,128)(2,1)S(1)}, bf16[4,128,2,1,128]{4,2,1,0,3:T(2,128)(2,1)S(1)}) fusion(bf16[4,128,2,1,128]{4,2,1,0,3:T(2,128)(2,1)S(1)} %squeeze.31, pred[4,128]{1,0:T(4,128)(4,1)S(1)} %add_compare_fusion.2, bf16[4,128,2,1,128]{4,2,1,0,3:T(2,128)(2,1)S(1)} %squeeze.32), kind=kLoop, calls=%fused_computation.25.clone.1 | loop fusion | flops 262144 | bytes 1049088 | tf_op jit(solution)/shard_map/while/body/eval_jaxpr/jit(_where)/select_n | solution.py:86
  44.9 0.7 pad_maximum_fusion.2
  46.9 9.3 %conditional.3 = ((f32[2,8,256]{2,1,0:T(8,128)S(1)}, f32[2,8,256]{2,1,0:T(8,128)S(1)}, f32[2,8,256,128]{3,2,1,0:T(8,128)})) conditional(s32[]{:T(128)} %convert_element_type.41, (f32[2,8,256]{2,1,0:T(8,128)S(1)}, f32[2,8,256]{2,1,0:T(8,128)S(1)}, f32[2,8,256,128]{3,2,1,0:T(8,128)}) %tuple.62, (s32[]{:T(128)}, s32[]{:T(128)}, s32[]{:T(128)}, ...), branch_computations={%region_4.4_spmd, %region_5.7_spmd} | conditional | flops 1102325504 | bytes 49553512 | solution.py:137
  48.0 1.4 %fusion.2 = (f32[2,8,256]{2,1,0:T(8,128)S(1)}, f32[2,512,256,8]{2,1,3,0:T(8,128)S(1)}) fusion(pred[256,512]{0,1:T(8,128)(4,1)S(1)} %compare_and_fusion, bf16[256,2,8,128]{3,0,2,1:T(8,128)(2,1)S(1)} %get-tuple-element.235, bf16[512,2,128,1]{2,1,0,3:T(2,128)(2,1)S(1)} %bitcast.45), kind=kOutput, calls=%fused_computation.4 | convolution fusion | flops 543158272 | bytes 9846784 | tf_op jit(solution)/shard_map/while/body/eval_jaxpr/cond/branch_1_fun/rkgd,pkd->kgrp/dot_general | solution.py:27
  49.4 2.0 %fusion.4 = f32[2,8,256]{2,1,0:T(8,128)S(1)} fusion(f32[2,512,256,8]{2,1,3,0:T(8,128)S(1)} %get-tuple-element.398, f32[2,8,256]{2,1,0:T(8,128)S(1)} %max.6, pred[256,512]{0,1:T(8,128)(4,1)S(1)} %compare_and_fusion), kind=kLoop, calls=%fused_computation.6 | loop fusion | flops 10481664 | bytes 8552448 | tf_op jit(solution)/shard_map/while/body/eval_jaxpr/cond/branch_1_fun/reduce_sum | solution.py:38
  51.4 3.4 %multiply_add_fusion = f32[2,8,256,128]{3,2,1,0:T(8,128)S(1)} fusion(f32[2,8,256,128]{3,2,1,0:T(8,128)S(1)} %copy-done, f32[2,512,256,8]{2,1,3,0:T(8,128)S(1)} %get-tuple-element.398, f32[2,8,256]{2,1,0:T(8,128)S(1)} %max.6, pred[256,512]{0,1:T(8,128)(4,1)S(1)} %compare_and_fusion, f32[2,8,256]{2,1,0:T(8,128)S(1)} %get-tuple-element.396, ...), kind=kOutput, calls=%fused_computation.9 | convolution fusion | flops 548405248 | bytes 13008896 | tf_op jit(solution)/shard_map/while/body/eval_jaxpr/cond/branch_1_fun/kgrp,pkd->kgrd/dot_general | solution.py:39
  54.9 1.3 %copy-done.1 = f32[2,8,256,128]{3,2,1,0:T(8,128)} copy-done((f32[2,8,256,128]{3,2,1,0:T(8,128)}, f32[2,8,256,128]{3,2,1,0:T(8,128)S(1)}, u32[]{:S(2)}) %copy-start.1) | copy-done | bytes 2097176 | tf_op jit(solution)/shard_map/while/body/eval_jaxpr/cond
  58.3 1.1 %constant_dynamic-slice_fusion.3 = (bf16[1,512,256]{2,1,0:T(8,128)(2,1)S(1)}, bf16[1,512,256]{2,1,0:T(8,128)(2,1)S(1)}) fusion(bf16[2,512,256]{2,1,0:T(8,128)(2,1)} %get-tuple-element.556, s32[]{:T(128)S(6)} %copy.67, bf16[2,512,256]{2,1,0:T(8,128)(2,1)} %get-tuple-element.555), kind=kLoop, calls=%fused_computation.31.clone.1 | loop fusion | bytes 1048580 | tf_op jit(solution)/shard_map/while/body/jit(dynamic_index_in_dim)/dynamic_slice | solution.py:157
  59.5 1.1 %broadcast_select_fusion.4 = (bf16[4,128,2,1,128]{4,2,1,0,3:T(2,128)(2,1)S(1)}, bf16[4,128,2,1,128]{4,2,1,0,3:T(2,128)(2,1)S(1)}) fusion(bf16[4,128,2,1,128]{4,2,1,0,3:T(2,128)(2,1)S(1)} %squeeze.31, pred[4,128]{1,0:T(4,128)(4,1)S(1)} %add_compare_fusion.2, bf16[4,128,2,1,128]{4,2,1,0,3:T(2,128)(2,1)S(1)} %squeeze.32), kind=kLoop, calls=%fused_computation.25.clone.1 | loop fusion | flops 262144 | bytes 1049088 | tf_op jit(solution)/shard_map/while/body/eval_jaxpr/jit(_where)/select_n | solution.py:86
  62.7 9.3 %conditional.3 = ((f32[2,8,256]{2,1,0:T(8,128)S(1)}, f32[2,8,256]{2,1,0:T(8,128)S(1)}, f32[2,8,256,128]{3,2,1,0:T(8,128)})) conditional(s32[]{:T(128)} %convert_element_type.41, (f32[2,8,256]{2,1,0:T(8,128)S(1)}, f32[2,8,256]{2,1,0:T(8,128)S(1)}, f32[2,8,256,128]{3,2,1,0:T(8,128)}) %tuple.62, (s32[]{:T(128)}, s32[]{:T(128)}, s32[]{:T(128)}, ...), branch_computations={%region_4.4_spmd, %region_5.7_spmd} | conditional | flops 1102325504 | bytes 49553512 | solution.py:137
  63.7 1.4 %fusion.2 = (f32[2,8,256]{2,1,0:T(8,128)S(1)}, f32[2,512,256,8]{2,1,3,0:T(8,128)S(1)}) fusion(pred[256,512]{0,1:T(8,128)(4,1)S(1)} %compare_and_fusion, bf16[256,2,8,128]{3,0,2,1:T(8,128)(2,1)S(1)} %get-tuple-element.235, bf16[512,2,128,1]{2,1,0,3:T(2,128)(2,1)S(1)} %bitcast.45), kind=kOutput, calls=%fused_computation.4 | convolution fusion | flops 543158272 | bytes 9846784 | tf_op jit(solution)/shard_map/while/body/eval_jaxpr/cond/branch_1_fun/rkgd,pkd->kgrp/dot_general | solution.py:27
  65.2 2.0 %fusion.4 = f32[2,8,256]{2,1,0:T(8,128)S(1)} fusion(f32[2,512,256,8]{2,1,3,0:T(8,128)S(1)} %get-tuple-element.398, f32[2,8,256]{2,1,0:T(8,128)S(1)} %max.6, pred[256,512]{0,1:T(8,128)(4,1)S(1)} %compare_and_fusion), kind=kLoop, calls=%fused_computation.6 | loop fusion | flops 10481664 | bytes 8552448 | tf_op jit(solution)/shard_map/while/body/eval_jaxpr/cond/branch_1_fun/reduce_sum | solution.py:38
  67.2 3.4 %multiply_add_fusion = f32[2,8,256,128]{3,2,1,0:T(8,128)S(1)} fusion(f32[2,8,256,128]{3,2,1,0:T(8,128)S(1)} %copy-done, f32[2,512,256,8]{2,1,3,0:T(8,128)S(1)} %get-tuple-element.398, f32[2,8,256]{2,1,0:T(8,128)S(1)} %max.6, pred[256,512]{0,1:T(8,128)(4,1)S(1)} %compare_and_fusion, f32[2,8,256]{2,1,0:T(8,128)S(1)} %get-tuple-element.396, ...), kind=kOutput, calls=%fused_computation.9 | convolution fusion | flops 548405248 | bytes 13008896 | tf_op jit(solution)/shard_map/while/body/eval_jaxpr/cond/branch_1_fun/kgrp,pkd->kgrd/dot_general | solution.py:39
  70.6 1.3 %copy-done.1 = f32[2,8,256,128]{3,2,1,0:T(8,128)} copy-done((f32[2,8,256,128]{3,2,1,0:T(8,128)}, f32[2,8,256,128]{3,2,1,0:T(8,128)S(1)}, u32[]{:S(2)}) %copy-start.1) | copy-done | bytes 2097176 | tf_op jit(solution)/shard_map/while/body/eval_jaxpr/cond
  72.0 2.0 %fusion.17 = bf16[256,2,8,128]{3,0,2,1:T(8,128)(2,1)S(1)} fusion(f32[2,8,256,128]{3,2,1,0:T(8,128)} %get-tuple-element.262, f32[2,8,256]{2,1,0:T(8,128)S(1)} %broadcast_select_fusion.2, pred[256]{0:T(512)(128)(4,1)S(1)} %broadcast_compare_fusion.1), kind=kLoop, calls=%fused_computation.35 | loop fusion | flops 1572864 | bytes 3162368 | tf_op jit(solution)/shard_map/convert_element_type | solution.py:53
  74.7 1.2 %copy.53 = bf16[32,8,16,128]{3,1,2,0:T(8,128)(2,1)} copy(bf16[32,8,16,128]{3,2,1,0:T(8,128)(2,1)S(1)} %bitcast.47) | data formatting | bytes 2097152
  75.9 1.0 %copy.37 = bf16[4,128,512]{2,1,0:T(8,128)(2,1)} copy(bf16[4,128,512]{1,2,0:T(8,128)(2,1)S(1)} %get-tuple-element.363) | data formatting | bytes 1048576
  (62 shorter events, 10.8 us)
Async XLA Ops:
  47.9 3.5 %copy-start = (f32[2,8,256,128]{3,2,1,0:T(8,128)S(1)}, f32[2,8,256,128]{3,2,1,0:T(8,128)}, u32[]{:S(2)}) copy-start(f32[2,8,256,128]{3,2,1,0:T(8,128)} %get-tuple-element.237) | copy-start | bytes 6291460 | tf_op jit(solution)/shard_map/while/body/eval_jaxpr/cond
  54.8 1.4 %copy-start.1 = (f32[2,8,256,128]{3,2,1,0:T(8,128)}, f32[2,8,256,128]{3,2,1,0:T(8,128)S(1)}, u32[]{:S(2)}) copy-start(f32[2,8,256,128]{3,2,1,0:T(8,128)S(1)} %multiply_add_fusion) | copy-start | bytes 6291460 | tf_op jit(solution)/shard_map/while/body/eval_jaxpr/cond
  63.7 3.5 %copy-start = (f32[2,8,256,128]{3,2,1,0:T(8,128)S(1)}, f32[2,8,256,128]{3,2,1,0:T(8,128)}, u32[]{:S(2)}) copy-start(f32[2,8,256,128]{3,2,1,0:T(8,128)} %get-tuple-element.237) | copy-start | bytes 6291460 | tf_op jit(solution)/shard_map/while/body/eval_jaxpr/cond
  70.6 1.4 %copy-start.1 = (f32[2,8,256,128]{3,2,1,0:T(8,128)}, f32[2,8,256,128]{3,2,1,0:T(8,128)S(1)}, u32[]{:S(2)}) copy-start(f32[2,8,256,128]{3,2,1,0:T(8,128)S(1)} %multiply_add_fusion) | copy-start | bytes 6291460 | tf_op jit(solution)/shard_map/while/body/eval_jaxpr/cond
where the time goes:
time: 77.3 us; the launch traced here: 76.9 us
  blocking collectives  32.7 us (42%)
  local copies, waits for them, and re-layouts  17.1 us (22%)
  other arithmetic  13.6 us (18%)
  matrix products  9.64 us (12%)
  between operations  2.06 us (3%)
  loops' own time  1.84 us (2%)
    all_gather x1, blocking collectives, local(): value_piece = lax.all_gather(values, 'seq', axis=0, tiled=True)  16.4 us
    all_gather x1, blocking collectives, local(): key_piece = lax.all_gather(keys, 'seq', axis=0, tiled=True)  16.3 us
    dot_general x2, matrix products, attend_block(): jnp.einsum('kgrp,pkd->kgrd', weights.astype(jnp.bfloat16), values_split,...  6.81 us
    unnamed x5, local copies, waits for them, and re-layouts  5.16 us
    reduce_sum x2, other arithmetic, attend_block(): denominator = query_state[1] * factor + jnp.sum(weights, axis=-1)  4.01 us
    dynamic_slice x4, local copies, waits for them, and re-layouts, local(): lax.scan(one_block, (states, page_store), (key_blocks, value_blocks, jnp....  3.47 us
    dot_general x2, matrix products, attend_block(): jnp.einsum('rkgd,pkd->kgrp', query_block, keys_split, preferred_element_t...  2.83 us
    cond x10, local copies, waits for them, and re-layouts  2.71 us

commit v1 on v0

--- a/solution.py
+++ b/solution.py
@@ -115,7 +115,9 @@
         (blank_state(kv_heads, group_size, part_rows.shape[0]) for part_rows in query_parts)
     )
     page_store = jnp.zeros((slots, PAGE_TOKENS, 2 * kv_width), jnp.bfloat16)
-    key_piece = lax.all_gather(keys, "seq", axis=0, tiled=True)
+    key_piece = jnp.concatenate(
+        lax.all_to_all(jnp.stack([keys] * lax.axis_size("seq")), "seq", 0, 0), axis=0
+    )
     value_piece = lax.all_gather(values, "seq", axis=0, tiled=True)
     block_count = key_piece.shape[0] // shard_rows
     per_step = max(1, min(block_count, 512 // shard_rows))

time: 77.3 us -> 70.3 us (0.909)
  blocking collectives: 32.7 us -> 19.3 us
  starting transfers between devices: 0 us -> 5.09 us
  local copies, waits for them, and re-layouts: 17.1 us -> 18.6 us
    all_gather x1 -> x0, blocking collectives: 16.3 us -> none  [local(): key_piece = lax.all_gather(keys, 'seq', axis=0, tiled=True)]
    all_to_all x0 -> x1, starting transfers between devices: none -> 5.09 us  [local(): lax.all_to_all(jnp.stack([keys] * lax.axis_size('seq')), 'seq', 0, 0)]
    all_gather x1, blocking collectives: 16.4 us -> 19.3 us  [local(): value_piece = lax.all_gather(values, 'seq', axis=0, tiled=True)]
    another operation x0 -> x1, local copies, waits for them, and re-layouts: none -> 1.73 us  [local(): jnp.stack([keys] * lax.axis_size('seq'))]
  transfers between devices with their start and end apart: 0 -> 1, of which waited for: 0 -> 0; matrix products, arithmetic and copies ran while one was open for 0% -> 6% of each run, Pallas kernels for 0% -> 0%
where the time goes in v1:
time: 70.3 us; the launch traced here: 69.9 us
  blocking collectives  19.3 us (27%)
  local copies, waits for them, and re-layouts  18.6 us (26%)
  other arithmetic  13.6 us (19%)
  matrix products  9.64 us (14%)
  starting transfers between devices  5.09 us (7%)
  between operations  1.98 us (3%)
  loops' own time  1.76 us (3%)
    all_gather x1, blocking collectives, local(): value_piece = lax.all_gather(values, 'seq', axis=0, tiled=True)  19.3 us
    dot_general x2, matrix products, attend_block(): jnp.einsum('kgrp,pkd->kgrd', weights.astype(jnp.bfloat16), values_split,...  6.81 us
    unnamed x5, local copies, waits for them, and re-layouts  5.15 us
    all_to_all x1, starting transfers between devices, local(): lax.all_to_all(jnp.stack([keys] * lax.axis_size('seq')), 'seq', 0, 0)  5.09 us
    reduce_sum x2, other arithmetic, attend_block(): denominator = query_state[1] * factor + jnp.sum(weights, axis=-1)  4.01 us
    dynamic_slice x4, local copies, waits for them, and re-layouts, local(): lax.scan(one_block, (states, page_store), (key_blocks, value_blocks, jnp....  3.31 us
    dot_general x2, matrix products, attend_block(): jnp.einsum('rkgd,pkd->kgrp', query_block, keys_split, preferred_element_t...  2.83 us
    cond x10, local copies, waits for them, and re-layouts  2.71 us
  transfers between devices with their start and end apart: 1, of which 0 were waited for; matrix products, arithmetic and copies ran while one was open for 6% of the time, Pallas kernels for 0%

profile of v1, /device:TPU:26, one launch (start us, length us, event | category | flops | bytes accessed | tf_op | source)
XLA Modules:
  0.0 69.9 jit_solution(9566404904997903782)
XLA Ops:
  0.6 1.7 %stack.14 = bf16[4,256,256]{2,1,0:T(8,128)(2,1)} broadcast(bf16[256,256]{1,0:T(8,128)(2,1)} %param.10), dimensions={1,2} | broadcast | bytes 655360 | tf_op jit(solution)/shard_map/stack | solution.py:119
  2.4 5.1 %all-to-all-start = ((bf16[4,256,256]{2,1,0:T(8,128)(2,1)}), bf16[4,256,256]{2,1,0:T(8,128)(2,1)}, u32[]{:S(2)}, u32[]{:S(2)}) async-start(bf16[4,256,256]{2,1,0:T(8,128)(2,1)} %stack.14), calls=%async_computation | async-start | bytes 1048576 | tf_op jit(solution)/shard_map/all_to_all | solution.py:119
  8.7 0.8 %copy.34 = s32[4,2]{1,0:T(4,128)S(1)} copy(s32[4,2]{0,1:T(2,128)} %param.13) | data formatting | bytes 64 | tf_op args[4]
  9.6 1.5 %copy.33 = bf16[256,2048]{0,1:T(8,128)(2,1)S(1)} copy(bf16[256,2048]{1,0:T(8,128)(2,1)} %param.9) | data formatting | bytes 2097152 | tf_op args[0]
  12.8 19.3 %all_gather.3 = bf16[1024,256]{1,0:T(8,128)(2,1)} all-gather(bf16[256,256]{1,0:T(8,128)(2,1)} %param.11), channel_id=1, replica_groups=mesh['groups'=2,'seq'=4,'head'=4] {'seq'}, dimensions={0}, use_global_device_ids=true | all-gather | bytes 655360 | tf_op jit(solution)/shard_map/all_gather | solution.py:121
  32.1 1.6 %broadcast_in_dim.106 = f32[2,8,256,128]{3,2,1,0:T(8,128)} broadcast(f32[]{:T(128)} %constant.102.clone.1), dimensions={} | broadcast | bytes 2097156 | tf_op jit(solution)/shard_map/broadcast_in_dim | solution.py:16
  33.6 31.3 %while.20 = (s32[]{:T(128)}, f32[2,8,256]{2,1,0:T(8,128)S(1)}, f32[2,8,256]{2,1,0:T(8,128)S(1)}, f32[2,8,256,128]{3,2,1,0:T(8,128)}, bf16[4,128,512]{1,2,0:T(8,1...) while((s32[]{:T(128)}, f32[2,8,256]{2,1,0:T(8,128)S(1)}, ...), condition=%wide.region_8.9_spmd.clone, body=%wide.region_3.8_spmd.clone.sunk | while | flops 1103377152 | bytes 57424572 | solution.py:159
  35.6 1.1 %constant_dynamic-slice_fusion.3 = (bf16[1,512,256]{2,1,0:T(8,128)(2,1)S(1)}, bf16[1,512,256]{2,1,0:T(8,128)(2,1)S(1)}) fusion(bf16[2,512,256]{2,1,0:T(8,128)(2,1)} %get-tuple-element.556, s32[]{:T(128)S(6)} %copy.67, bf16[2,512,256]{2,1,0:T(8,128)(2,1)} %get-tuple-element.555), kind=kLoop, calls=%fused_computation.31.clone.1 | loop fusion | bytes 1048580 | tf_op jit(solution)/shard_map/while/body/jit(dynamic_index_in_dim)/dynamic_slice | solution.py:159
  36.8 1.1 %broadcast_select_fusion.4 = (bf16[4,128,2,1,128]{4,2,1,0,3:T(2,128)(2,1)S(1)}, bf16[4,128,2,1,128]{4,2,1,0,3:T(2,128)(2,1)S(1)}) fusion(bf16[4,128,2,1,128]{4,2,1,0,3:T(2,128)(2,1)S(1)} %squeeze.31, pred[4,128]{1,0:T(4,128)(4,1)S(1)} %add_compare_fusion.2, bf16[4,128,2,1,128]{4,2,1,0,3:T(2,128)(2,1)S(1)} %squeeze.32), kind=kLoop, calls=%fused_computation.25.clone.1 | loop fusion | flops 262144 | bytes 1049088 | tf_op jit(solution)/shard_map/while/body/eval_jaxpr/jit(_where)/select_n | solution.py:86
  40.0 9.3 %conditional.3 = ((f32[2,8,256]{2,1,0:T(8,128)S(1)}, f32[2,8,256]{2,1,0:T(8,128)S(1)}, f32[2,8,256,128]{3,2,1,0:T(8,128)})) conditional(s32[]{:T(128)} %convert_element_type.41, (f32[2,8,256]{2,1,0:T(8,128)S(1)}, f32[2,8,256]{2,1,0:T(8,128)S(1)}, f32[2,8,256,128]{3,2,1,0:T(8,128)}) %tuple.62, (s32[]{:T(128)}, s32[]{:T(128)}, s32[]{:T(128)}, ...), branch_computations={%region_4.4_spmd, %region_5.7_spmd} | conditional | flops 1102325504 | bytes 49553512 | solution.py:139
  41.0 1.4 %fusion.2 = (f32[2,8,256]{2,1,0:T(8,128)S(1)}, f32[2,512,256,8]{2,1,3,0:T(8,128)S(1)}) fusion(pred[256,512]{0,1:T(8,128)(4,1)S(1)} %compare_and_fusion, bf16[256,2,8,128]{3,0,2,1:T(8,128)(2,1)S(1)} %get-tuple-element.235, bf16[512,2,128,1]{2,1,0,3:T(2,128)(2,1)S(1)} %bitcast.45), kind=kOutput, calls=%fused_computation.4 | convolution fusion | flops 543158272 | bytes 9846784 | tf_op jit(solution)/shard_map/while/body/eval_jaxpr/cond/branch_1_fun/rkgd,pkd->kgrp/dot_general | solution.py:27
  42.5 2.0 %fusion.4 = f32[2,8,256]{2,1,0:T(8,128)S(1)} fusion(f32[2,512,256,8]{2,1,3,0:T(8,128)S(1)} %get-tuple-element.398, f32[2,8,256]{2,1,0:T(8,128)S(1)} %max.6, pred[256,512]{0,1:T(8,128)(4,1)S(1)} %compare_and_fusion), kind=kLoop, calls=%fused_computation.6 | loop fusion | flops 10481664 | bytes 8552448 | tf_op jit(solution)/shard_map/while/body/eval_jaxpr/cond/branch_1_fun/reduce_sum | solution.py:38
  44.5 3.4 %multiply_add_fusion = f32[2,8,256,128]{3,2,1,0:T(8,128)S(1)} fusion(f32[2,8,256,128]{3,2,1,0:T(8,128)S(1)} %copy-done, f32[2,512,256,8]{2,1,3,0:T(8,128)S(1)} %get-tuple-element.398, f32[2,8,256]{2,1,0:T(8,128)S(1)} %max.6, pred[256,512]{0,1:T(8,128)(4,1)S(1)} %compare_and_fusion, f32[2,8,256]{2,1,0:T(8,128)S(1)} %get-tuple-element.396, ...), kind=kOutput, calls=%fused_computation.9 | convolution fusion | flops 548405248 | bytes 13008896 | tf_op jit(solution)/shard_map/while/body/eval_jaxpr/cond/branch_1_fun/kgrp,pkd->kgrd/dot_general | solution.py:39
  47.9 1.3 %copy-done.1 = f32[2,8,256,128]{3,2,1,0:T(8,128)} copy-done((f32[2,8,256,128]{3,2,1,0:T(8,128)}, f32[2,8,256,128]{3,2,1,0:T(8,128)S(1)}, u32[]{:S(2)}) %copy-start.1) | copy-done | bytes 2097176 | tf_op jit(solution)/shard_map/while/body/eval_jaxpr/cond
  51.3 1.1 %constant_dynamic-slice_fusion.3 = (bf16[1,512,256]{2,1,0:T(8,128)(2,1)S(1)}, bf16[1,512,256]{2,1,0:T(8,128)(2,1)S(1)}) fusion(bf16[2,512,256]{2,1,0:T(8,128)(2,1)} %get-tuple-element.556, s32[]{:T(128)S(6)} %copy.67, bf16[2,512,256]{2,1,0:T(8,128)(2,1)} %get-tuple-element.555), kind=kLoop, calls=%fused_computation.31.clone.1 | loop fusion | bytes 1048580 | tf_op jit(solution)/shard_map/while/body/jit(dynamic_index_in_dim)/dynamic_slice | solution.py:159
  52.5 1.1 %broadcast_select_fusion.4 = (bf16[4,128,2,1,128]{4,2,1,0,3:T(2,128)(2,1)S(1)}, bf16[4,128,2,1,128]{4,2,1,0,3:T(2,128)(2,1)S(1)}) fusion(bf16[4,128,2,1,128]{4,2,1,0,3:T(2,128)(2,1)S(1)} %squeeze.31, pred[4,128]{1,0:T(4,128)(4,1)S(1)} %add_compare_fusion.2, bf16[4,128,2,1,128]{4,2,1,0,3:T(2,128)(2,1)S(1)} %squeeze.32), kind=kLoop, calls=%fused_computation.25.clone.1 | loop fusion | flops 262144 | bytes 1049088 | tf_op jit(solution)/shard_map/while/body/eval_jaxpr/jit(_where)/select_n | solution.py:86
  55.6 9.3 %conditional.3 = ((f32[2,8,256]{2,1,0:T(8,128)S(1)}, f32[2,8,256]{2,1,0:T(8,128)S(1)}, f32[2,8,256,128]{3,2,1,0:T(8,128)})) conditional(s32[]{:T(128)} %convert_element_type.41, (f32[2,8,256]{2,1,0:T(8,128)S(1)}, f32[2,8,256]{2,1,0:T(8,128)S(1)}, f32[2,8,256,128]{3,2,1,0:T(8,128)}) %tuple.62, (s32[]{:T(128)}, s32[]{:T(128)}, s32[]{:T(128)}, ...), branch_computations={%region_4.4_spmd, %region_5.7_spmd} | conditional | flops 1102325504 | bytes 49553512 | solution.py:139
  56.7 1.4 %fusion.2 = (f32[2,8,256]{2,1,0:T(8,128)S(1)}, f32[2,512,256,8]{2,1,3,0:T(8,128)S(1)}) fusion(pred[256,512]{0,1:T(8,128)(4,1)S(1)} %compare_and_fusion, bf16[256,2,8,128]{3,0,2,1:T(8,128)(2,1)S(1)} %get-tuple-element.235, bf16[512,2,128,1]{2,1,0,3:T(2,128)(2,1)S(1)} %bitcast.45), kind=kOutput, calls=%fused_computation.4 | convolution fusion | flops 543158272 | bytes 9846784 | tf_op jit(solution)/shard_map/while/body/eval_jaxpr/cond/branch_1_fun/rkgd,pkd->kgrp/dot_general | solution.py:27
  58.1 2.0 %fusion.4 = f32[2,8,256]{2,1,0:T(8,128)S(1)} fusion(f32[2,512,256,8]{2,1,3,0:T(8,128)S(1)} %get-tuple-element.398, f32[2,8,256]{2,1,0:T(8,128)S(1)} %max.6, pred[256,512]{0,1:T(8,128)(4,1)S(1)} %compare_and_fusion), kind=kLoop, calls=%fused_computation.6 | loop fusion | flops 10481664 | bytes 8552448 | tf_op jit(solution)/shard_map/while/body/eval_jaxpr/cond/branch_1_fun/reduce_sum | solution.py:38
  60.2 3.4 %multiply_add_fusion = f32[2,8,256,128]{3,2,1,0:T(8,128)S(1)} fusion(f32[2,8,256,128]{3,2,1,0:T(8,128)S(1)} %copy-done, f32[2,512,256,8]{2,1,3,0:T(8,128)S(1)} %get-tuple-element.398, f32[2,8,256]{2,1,0:T(8,128)S(1)} %max.6, pred[256,512]{0,1:T(8,128)(4,1)S(1)} %compare_and_fusion, f32[2,8,256]{2,1,0:T(8,128)S(1)} %get-tuple-element.396, ...), kind=kOutput, calls=%fused_computation.9 | convolution fusion | flops 548405248 | bytes 13008896 | tf_op jit(solution)/shard_map/while/body/eval_jaxpr/cond/branch_1_fun/kgrp,pkd->kgrd/dot_general | solution.py:39
  63.6 1.3 %copy-done.1 = f32[2,8,256,128]{3,2,1,0:T(8,128)} copy-done((f32[2,8,256,128]{3,2,1,0:T(8,128)}, f32[2,8,256,128]{3,2,1,0:T(8,128)S(1)}, u32[]{:S(2)}) %copy-start.1) | copy-done | bytes 2097176 | tf_op jit(solution)/shard_map/while/body/eval_jaxpr/cond
  64.9 2.0 %fusion.17 = bf16[256,2,8,128]{3,0,2,1:T(8,128)(2,1)S(1)} fusion(f32[2,8,256,128]{3,2,1,0:T(8,128)} %get-tuple-element.262, f32[2,8,256]{2,1,0:T(8,128)S(1)} %broadcast_select_fusion.2, pred[256]{0:T(512)(128)(4,1)S(1)} %broadcast_compare_fusion.1), kind=kLoop, calls=%fused_computation.35 | loop fusion | flops 1572864 | bytes 3162368 | tf_op jit(solution)/shard_map/convert_element_type | solution.py:53
  67.6 1.2 %copy.53 = bf16[32,8,16,128]{3,1,2,0:T(8,128)(2,1)} copy(bf16[32,8,16,128]{3,2,1,0:T(8,128)(2,1)S(1)} %bitcast.47) | data formatting | bytes 2097152
  68.9 1.0 %copy.37 = bf16[4,128,512]{2,1,0:T(8,128)(2,1)} copy(bf16[4,128,512]{1,2,0:T(8,128)(2,1)S(1)} %get-tuple-element.363) | data formatting | bytes 1048576
  (64 shorter events, 11.3 us)
Async XLA Ops:
  2.4 29.7 %all-to-all-start = ((bf16[4,256,256]{2,1,0:T(8,128)(2,1)}), bf16[4,256,256]{2,1,0:T(8,128)(2,1)}, u32[]{:S(2)}, u32[]{:S(2)}) async-start(bf16[4,256,256]{2,1,0:T(8,128)(2,1)} %stack.14), calls=%async_computation | async-start | bytes 1048576 | tf_op jit(solution)/shard_map/all_to_all | solution.py:119
  41.0 3.5 %copy-start = (f32[2,8,256,128]{3,2,1,0:T(8,128)S(1)}, f32[2,8,256,128]{3,2,1,0:T(8,128)}, u32[]{:S(2)}) copy-start(f32[2,8,256,128]{3,2,1,0:T(8,128)} %get-tuple-element.237) | copy-start | bytes 6291460 | tf_op jit(solution)/shard_map/while/body/eval_jaxpr/cond
  47.9 1.4 %copy-start.1 = (f32[2,8,256,128]{3,2,1,0:T(8,128)}, f32[2,8,256,128]{3,2,1,0:T(8,128)S(1)}, u32[]{:S(2)}) copy-start(f32[2,8,256,128]{3,2,1,0:T(8,128)S(1)} %multiply_add_fusion) | copy-start | bytes 6291460 | tf_op jit(solution)/shard_map/while/body/eval_jaxpr/cond
  56.7 3.5 %copy-start = (f32[2,8,256,128]{3,2,1,0:T(8,128)S(1)}, f32[2,8,256,128]{3,2,1,0:T(8,128)}, u32[]{:S(2)}) copy-start(f32[2,8,256,128]{3,2,1,0:T(8,128)} %get-tuple-element.237) | copy-start | bytes 6291460 | tf_op jit(solution)/shard_map/while/body/eval_jaxpr/cond
  63.6 1.4 %copy-start.1 = (f32[2,8,256,128]{3,2,1,0:T(8,128)}, f32[2,8,256,128]{3,2,1,0:T(8,128)S(1)}, u32[]{:S(2)}) copy-start(f32[2,8,256,128]{3,2,1,0:T(8,128)S(1)} %multiply_add_fusion) | copy-start | bytes 6291460 | tf_op jit(solution)/shard_map/while/body/eval_jaxpr/cond
